TPU v7x, 32 devices: a whole 2x2x4 slice. The times are simulated.
32 devices in a mesh: gx: 2 (over y), gy: 4 (over x, core), gz: 4 (over z).
Axes of the slice: x: 2, y: 2, z: 4, core: 2. Of those that a mesh axis runs over, the one named last changes fastest.
Arguments:
- loads: float32 [16, 4, 16, 1024], P(None, 'gx', 'gy', 'gz'), may hold values from -60 to 60
- moduli: float32 [8], replicated, may hold values from 0.5 to 4
- material: int32 [4, 16, 1024], P('gx', 'gy', 'gz'), may hold values from 0 to 7
Outputs:
- solution: float32 [16, 4, 16, 1024], P(None, 'gx', 'gy', 'gz')
- residual: float32 [16, 4, 16, 1024], P(None, 'gx', 'gy', 'gz')
All inputs are finite; a program needn't handle non-finite values.
Results may differ from a plain program's by a relative error of at most 0.005.
The roundings to bfloat16 on the way count: a program that leaves them out, or rounds other values in their place, can miss the bound.
Values may be sent and summed in bfloat16 or wider, within the bound.
A program may use at most 64 MiB of HBM per device.

v0:
```python
import jax
import jax.numpy as jnp
import numpy as np
from jax import lax
from jax.sharding import PartitionSpec as P

ITERS = 2
SIGMA = 0.25


def padded_2(cells, sides, width):
    for axis, dim in sides:
        count = lax.axis_size(axis)
        ends = count - 1
        head = lax.slice_in_dim(cells, 0, width, axis=dim)
        tail = lax.slice_in_dim(cells, cells.shape[dim] - width, cells.shape[dim], axis=dim)
        cells = jnp.concatenate(
            [
                lax.ppermute(tail, axis, [(i, (i + 1) % count) for i in range(ends)]),
                cells,
                lax.ppermute(head, axis, [((i + 1) % count, i) for i in range(ends)]),
            ],
            axis=dim,
        )
    return cells


def stiffness_table():
    line_mass = np.array([[1.0 / 3.0, 1.0 / 6.0], [1.0 / 6.0, 1.0 / 3.0]])
    line_stiff = np.array([[1.0, -1.0], [-1.0, 1.0]])
    table = np.zeros((8, 8))
    for target in range(8):
        for source in range(8):
            target_bits = [target >> 2 & 1, target >> 1 & 1, target & 1]
            source_bits = [source >> 2 & 1, source >> 1 & 1, source & 1]
            total = 0.0
            for stiff_dim in range(3):
                factor = 1.0
                for other in range(3):
                    if other == stiff_dim:
                        factor = factor * line_stiff[target_bits[other], source_bits[other]]
                    else:
                        factor = factor * line_mass[target_bits[other], source_bits[other]]
                total = total + factor
            table[target, source] = total
    return table


def corner_bits(corner):
    return (corner >> 2 & 1, corner >> 1 & 1, corner & 1)


def apply_operator(field, weights, kernel):
    lowered = field.astype(jnp.bfloat16)
    padded = padded_2(lowered, (("gx", 1), ("gy", 2), ("gz", 3)), 1)
    size_x, size_y, size_z = (field.shape[1], field.shape[2], field.shape[3])
    pieces = []
    for corner in range(8):
        bit_x, bit_y, bit_z = corner_bits(corner)
        pieces.append(
            padded[
                :,
                bit_x : bit_x + size_x + 1,
                bit_y : bit_y + size_y + 1,
                bit_z : bit_z + size_z + 1,
            ]
        )
    stacked = jnp.stack(pieces)
    total = SIGMA * field
    for corner in range(8):
        bit_x, bit_y, bit_z = corner_bits(corner)
        part = (
            jnp.einsum("b,bcxyz->cxyz", kernel[corner], stacked, preferred_element_type=jnp.float32)
            * weights
        )
        total = (
            total
            + part[
                :,
                1 - bit_x : 1 - bit_x + size_x,
                1 - bit_y : 1 - bit_y + size_y,
                1 - bit_z : 1 - bit_z + size_z,
            ]
        )
    return total


def local_gram(left, right):
    return jnp.einsum("cxyz,dxyz->cd", left, right, precision=lax.Precision.HIGHEST)


def combine(block, coeffs):
    return jnp.einsum("cxyz,cd->dxyz", block, coeffs, precision=lax.Precision.HIGHEST)


def solve_small(matrix, rhs_small):
    factor = jnp.linalg.cholesky(matrix)
    return jax.scipy.linalg.cho_solve((factor, True), rhs_small)


def residual_gram(residual):
    return lax.psum(local_gram(residual, residual), ("gx", "gy", "gz"))


def on_device(loads, moduli, material):
    kernel = jnp.asarray(stiffness_table(), jnp.float32).astype(jnp.bfloat16)
    levels = jnp.arange(moduli.shape[0], dtype=jnp.int32)
    node_modulus = jnp.sum(jnp.where(material[..., None] == levels, moduli, 0.0), axis=-1)
    padded_mod = padded_2(node_modulus, (("gx", 0), ("gy", 1), ("gz", 2)), 1)
    size_x, size_y, size_z = material.shape
    weights = jnp.zeros((size_x + 1, size_y + 1, size_z + 1), jnp.float32)
    for corner in range(8):
        bit_x, bit_y, bit_z = corner_bits(corner)
        weights = (
            weights
            + padded_mod[
                bit_x : bit_x + size_x + 1, bit_y : bit_y + size_y + 1, bit_z : bit_z + size_z + 1
            ]
        )
    weights = weights * 0.125
    solution = jnp.zeros_like(loads)
    residual = loads
    direction = loads
    current = residual_gram(residual)
    for iteration in range(ITERS):
        image = apply_operator(direction, weights, kernel)
        curvature, cross, image_sq = lax.psum(
            (local_gram(direction, image), local_gram(image, residual), local_gram(image, image)),
            ("gx", "gy", "gz"),
        )
        alpha = solve_small(curvature, current)
        solution = solution + combine(direction, alpha)
        residual = residual - combine(image, alpha)
        if iteration + 1 < ITERS:
            high = lax.Precision.HIGHEST
            cross_term = jnp.dot(alpha.T, cross, precision=high)
            quad_term = jnp.dot(jnp.dot(alpha.T, image_sq, precision=high), alpha, precision=high)
            updated = current - cross_term - cross_term.T + quad_term
            beta = solve_small(current, updated)
            direction = residual + combine(direction, beta)
            current = updated
    return (solution, residual)


def solution(mesh):
    in_specs = (P(None, "gx", "gy", "gz"), P(), P("gx", "gy", "gz"))
    out_specs = (P(None, "gx", "gy", "gz"), P(None, "gx", "gy", "gz"))
    return jax.shard_map(
        on_device, mesh=mesh, in_specs=in_specs, out_specs=out_specs, check_vma=False
    )
```

profile of v0, /device:TPU:0, one launch (start us, length us, event | category | flops | bytes accessed | tf_op | source)
XLA Modules:
  0.0 185.7 jit_solution(12359744168205889732)
XLA Ops:
  0.6 0.8 select_reduce_fusion
  1.4 4.9 %collective-permute-start.6 = (f32[1,4,256]{2,1,0:T(4,128)S(1)}, f32[1,4,256]{2,1,0:T(4,128)S(1)}, u32[]{:S(2)}, u32[]{:S(2)}) collective-permute-start(f32[1,4,256]{2,1,0:T(4,128)S(1)} %get-tuple-element.42), channel_id=1, source_target_pairs={{0,16},{1,17},{2,18},{3,19},{4,20},{5,21},{6,22},{7,23},{8,24},{9,... | collective-permute-start | bytes 12296 | tf_op jit(solution)/shard_map/ppermute | solution.py:19
  6.4 1.3 collective-permute-start.7
  7.7 0.9 convert_element_type.9
  8.6 4.5 %collective-permute-start = (bf16[16,1,4,256]{3,2,1,0:T(4,128)(2,1)S(1)}, bf16[16,1,4,256]{3,2,1,0:T(4,128)(2,1)S(1)}, u32[]{:S(2)}, u32[]{:S(2)}) collective-permute-start(bf16[16,1,4,256]{3,2,1,0:T(4,128)(2,1)S(1)} %get-tuple-element.26), channel_id=1, source_target_pairs={{0,16},{1,17},{2,18},{3,19},{4,20},{5,21},{6,22},{7,23},{8,24},{9,... | collective-permute-start | bytes 98312 | tf_op jit(solution)/shard_map/ppermute | solution.py:19
  13.2 1.3 collective-permute-start.1
  14.5 1.3 collective-permute-start.8
  15.8 1.3 collective-permute-start.9
  17.1 1.3 convolution_bitcast_fusion.4
  18.4 2.2 %collective-permute-done.9 = f32[4,1,256]{2,1,0:T(1,128)S(1)} collective-permute-done((f32[4,1,256]{2,1,0:T(1,128)S(1)}, f32[4,1,256]{2,1,0:T(1,128)S(1)}, u32[]{:S(2)}, u32[]{:S(2)}) %collective-permute-start.9) | collective-permute-done | bytes 4128 | tf_op jit(solution)/shard_map/ppermute | solution.py:21
  20.7 3.5 %collective-permute-start.10 = (f32[4,6,1]{2,1,0:T(8,128)S(1)}, f32[4,6,1]{2,1,0:T(8,128)S(1)}, u32[]{:S(2)}, u32[]{:S(2)}) collective-permute-start(f32[4,6,1]{2,1,0:T(8,128)S(1)} %get-tuple-element.36), channel_id=1, source_target_pairs={{0,1},{1,2},{2,3},{4,5},{5,6},{6,7},{8,9},{9,10},{10,11},{12,13},{... | collective-permute-start | bytes 296 | tf_op jit(solution)/shard_map/ppermute | solution.py:19
  24.2 1.3 collective-permute-start.11
  25.6 4.2 %collective-permute-done.11 = f32[4,6,1]{2,1,0:T(8,128)S(1)} collective-permute-done((f32[4,6,1]{2,1,0:T(8,128)S(1)}, f32[4,6,1]{2,1,0:T(8,128)S(1)}, u32[]{:S(2)}, u32[]{:S(2)}) %collective-permute-start.11) | collective-permute-done | bytes 128 | tf_op jit(solution)/shard_map/ppermute | solution.py:21
  30.1 2.8 %collective-permute-start.2 = (bf16[16,4,1,256]{3,2,1,0:T(2,128)(2,1)S(1)}, bf16[16,4,1,256]{3,2,1,0:T(2,128)(2,1)S(1)}, u32[]{:S(2)}, u32[]{:S(2)}) collective-permute-start(bf16[16,4,1,256]{3,2,1,0:T(2,128)(2,1)S(1)} %get-tuple-element.22), channel_id=1, source_target_pairs={{0,4},{4,8},{8,12},{1,5},{5,9},{9,13},{2,6},{6,10},{10,14},{3,7},{... | collective-permute-start | bytes 98312 | tf_op jit(solution)/shard_map/ppermute | solution.py:19
  33.0 1.3 collective-permute-start.3
  34.3 2.8 %collective-permute-done.3 = bf16[16,4,1,256]{3,2,1,0:T(2,128)(2,1)S(1)} collective-permute-done((bf16[16,4,1,256]{3,2,1,0:T(2,128)(2,1)S(1)}, bf16[16,4,1,256]{3,2,1,0:T(2,128)(2,1)S(1)}, u32[]{:S(2)}, u32[]{:S(2)}) %collective-permute-start.3) | collective-permute-done | bytes 32800 | tf_op jit(solution)/shard_map/ppermute | solution.py:21
  37.5 3.5 %collective-permute-start.4 = (bf16[16,4,6,1]{3,2,1,0:T(8,128)(2,1)S(1)}, bf16[16,4,6,1]{3,2,1,0:T(8,128)(2,1)S(1)}, u32[]{:S(2)}, u32[]{:S(2)}) collective-permute-start(bf16[16,4,6,1]{3,2,1,0:T(8,128)(2,1)S(1)} %get-tuple-element.15), channel_id=1, source_target_pairs={{0,1},{1,2},{2,3},{4,5},{5,6},{6,7},{8,9},{9,10},{10,11},{12,13},{... | collective-permute-start | bytes 2312 | tf_op jit(solution)/shard_map/ppermute | solution.py:19
  41.0 1.3 collective-permute-start.5
  42.4 1.1 collective-permute-done.4
  43.5 4.4 %collective-permute-done.5 = bf16[16,4,6,1]{3,2,1,0:T(8,128)(2,1)S(1)} collective-permute-done((bf16[16,4,6,1]{3,2,1,0:T(8,128)(2,1)S(1)}, bf16[16,4,6,1]{3,2,1,0:T(8,128)(2,1)S(1)}, u32[]{:S(2)}, u32[]{:S(2)}) %collective-permute-start.5) | collective-permute-done | bytes 800 | tf_op jit(solution)/shard_map/ppermute | solution.py:21
  47.8 0.9 pad_maximum_fusion
  49.3 1.6 copy.46
  51.0 0.5 fusion.82
  51.6 0.5 fusion.83
  52.2 0.5 fusion.84
  52.7 0.5 fusion.85
  53.3 0.5 fusion.86
  53.8 0.5 fusion.87
  54.4 0.5 fusion.88
  54.9 0.5 fusion.89
  55.7 0.8 copy-done
  57.3 43.2 %all-reduce = (f32[16,16]{0,1:T(8,128)S(1)}, f32[16,16]{0,1:T(8,128)S(1)}, f32[16,16]{1,0:T(8,128)S(1)}, f32[16,16]{1,0:T(8,128)S(1)}) all-reduce(f32[16,16]{0,1:T(8,128)S(1)} %convolution_bitcast_fusion.4, f32[16,16]{0,1:T(8,128)S(1)} %bitcast.265, ...), channel_id=1, replica_groups=mesh['gx'=2,'gy'=4,'gz'=4] {'gx','gy','gz'}, use_global_device_ids=true, to_apply=%region_4.0 | all-reduce | flops 1024 | bytes 8192 | tf_op jit(solution)/shard_map/psum | solution.py:102
  100.6 1.5 cholesky.70
  102.1 0.6 compare_reduce_fusion.1
  102.8 0.6 fusion.56
  103.4 1.2 custom-call.10
  104.7 1.5 cholesky.59
  106.2 0.6 compare_reduce_fusion.2
  106.9 0.6 fusion.55
  107.5 1.2 custom-call.9
  110.8 4.2 %collective-permute-start.12 = (bf16[16,1,4,256]{3,0,2,1:T(8,128)(2,1)S(1)}, bf16[16,1,4,256]{3,0,2,1:T(8,128)(2,1)S(1)}, u32[]{:S(2)}, u32[]{:S(2)}) collective-permute-start(bf16[16,1,4,256]{3,0,2,1:T(8,128)(2,1)S(1)} %get-tuple-element.24), channel_id=1, source_target_pairs={{0,16},{1,17},{2,18},{3,19},{4,20},{5,21},{6,22},{7,23},{8,24},{9,... | collective-permute-start | bytes 98312 | tf_op jit(solution)/shard_map/ppermute | solution.py:19
  115.0 1.3 collective-permute-start.13
  116.6 4.2 %collective-permute-done.13 = bf16[16,1,4,256]{3,0,2,1:T(8,128)(2,1)S(1)} collective-permute-done((bf16[16,1,4,256]{3,0,2,1:T(8,128)(2,1)S(1)}, bf16[16,1,4,256]{3,0,2,1:T(8,128)(2,1)S(1)}, u32[]{:S(2)}, u32[]{:S(2)}) %collective-permute-start.13) | collective-permute-done | bytes 32800 | tf_op jit(solution)/shard_map/ppermute | solution.py:21
  120.8 1.3 collective-permute-start.14
  122.1 1.3 collective-permute-start.15
  123.5 2.1 %collective-permute-done.15 = bf16[16,4,1,256]{3,0,2,1:T(8,128)(2,1)S(1)} collective-permute-done((bf16[16,4,1,256]{3,0,2,1:T(8,128)(2,1)S(1)}, bf16[16,4,1,256]{3,0,2,1:T(8,128)(2,1)S(1)}, u32[]{:S(2)}, u32[]{:S(2)}) %collective-permute-start.15) | collective-permute-done | bytes 32800 | tf_op jit(solution)/shard_map/ppermute | solution.py:21
  125.7 2.3 %collective-permute-start.16 = (bf16[16,4,6,1]{3,0,2,1:T(8,128)(2,1)S(1)}, bf16[16,4,6,1]{3,0,2,1:T(8,128)(2,1)S(1)}, u32[]{:S(2)}, u32[]{:S(2)}) collective-permute-start(bf16[16,4,6,1]{3,0,2,1:T(8,128)(2,1)S(1)} %get-tuple-element.19), channel_id=1, source_target_pairs={{0,1},{1,2},{2,3},{4,5},{5,6},{6,7},{8,9},{9,10},{10,11},{12,13},{... | collective-permute-start | bytes 2312 | tf_op jit(solution)/shard_map/ppermute | solution.py:19
  128.1 1.3 collective-permute-start.17
  129.7 0.6 collective-permute-done.16
  130.3 4.3 %collective-permute-done.17 = bf16[16,4,6,1]{3,0,2,1:T(8,128)(2,1)S(1)} collective-permute-done((bf16[16,4,6,1]{3,0,2,1:T(8,128)(2,1)S(1)}, bf16[16,4,6,1]{3,0,2,1:T(8,128)(2,1)S(1)}, u32[]{:S(2)}, u32[]{:S(2)}) %collective-permute-start.17) | collective-permute-done | bytes 800 | tf_op jit(solution)/shard_map/ppermute | solution.py:21
  135.1 0.5 fusion.8
  135.6 0.5 fusion.10
  136.1 0.5 fusion.12
  137.2 0.5 fusion.16
  137.7 0.5 fusion.18
  138.2 0.5 fusion.20
  138.7 0.5 fusion.22
  140.0 39.1 %psum.39 = f32[16,16]{0,1:T(8,128)S(1)} all-reduce(f32[16,16]{0,1:T(8,128)S(1)} %convolution_bitcast_fusion.1), channel_id=1, replica_groups=mesh['gx'=2,'gy'=4,'gz'=4] {'gx','gy','gz'}, use_global_device_ids=true, to_apply=%region_7.10 | all-reduce | flops 256 | bytes 2048 | tf_op jit(solution)/shard_map/psum | solution.py:127
  179.3 1.5 cholesky.81
  180.7 0.6 compare_reduce_fusion
  181.4 0.6 fusion.57
  182.0 1.2 custom-call.11
  184.0 0.7 copy.45
  185.0 0.7 copy.44
  (101 shorter events, 8.5 us)
Async XLA Ops:
  1.4 13.0 %collective-permute-start.6 = (f32[1,4,256]{2,1,0:T(4,128)S(1)}, f32[1,4,256]{2,1,0:T(4,128)S(1)}, u32[]{:S(2)}, u32[]{:S(2)}) collective-permute-start(f32[1,4,256]{2,1,0:T(4,128)S(1)} %get-tuple-element.42), channel_id=1, source_target_pairs={{0,16},{1,17},{2,18},{3,19},{4,20},{5,21},{6,22},{7,23},{8,24},{9,... | collective-permute-start | bytes 12296 | tf_op jit(solution)/shard_map/ppermute | solution.py:19
  6.4 8.1 %collective-permute-start.7 = (f32[1,4,256]{2,1,0:T(4,128)S(1)}, f32[1,4,256]{2,1,0:T(4,128)S(1)}, u32[]{:S(2)}, u32[]{:S(2)}) collective-permute-start(f32[1,4,256]{2,1,0:T(4,128)S(1)} %get-tuple-element.43), channel_id=1, source_target_pairs={{16,0},{17,1},{18,2},{19,3},{20,4},{21,5},{22,6},{23,7},{24,8},{25... | collective-permute-start | bytes 12296 | tf_op jit(solution)/shard_map/ppermute | solution.py:21
  8.6 21.3 %collective-permute-start = (bf16[16,1,4,256]{3,2,1,0:T(4,128)(2,1)S(1)}, bf16[16,1,4,256]{3,2,1,0:T(4,128)(2,1)S(1)}, u32[]{:S(2)}, u32[]{:S(2)}) collective-permute-start(bf16[16,1,4,256]{3,2,1,0:T(4,128)(2,1)S(1)} %get-tuple-element.26), channel_id=1, source_target_pairs={{0,16},{1,17},{2,18},{3,19},{4,20},{5,21},{6,22},{7,23},{8,24},{9,... | collective-permute-start | bytes 98312 | tf_op jit(solution)/shard_map/ppermute | solution.py:19
  13.2 16.8 %collective-permute-start.1 = (bf16[16,1,4,256]{3,2,1,0:T(4,128)(2,1)S(1)}, bf16[16,1,4,256]{3,2,1,0:T(4,128)(2,1)S(1)}, u32[]{:S(2)}, u32[]{:S(2)}) collective-permute-start(bf16[16,1,4,256]{3,2,1,0:T(4,128)(2,1)S(1)} %get-tuple-element.27), channel_id=1, source_target_pairs={{16,0},{17,1},{18,2},{19,3},{20,4},{21,5},{22,6},{23,7},{24,8},{25... | collective-permute-start | bytes 98312 | tf_op jit(solution)/shard_map/ppermute | solution.py:21
  14.5 3.9 %collective-permute-start.8 = (f32[4,1,256]{2,1,0:T(1,128)S(1)}, f32[4,1,256]{2,1,0:T(1,128)S(1)}, u32[]{:S(2)}, u32[]{:S(2)}) collective-permute-start(f32[4,1,256]{2,1,0:T(1,128)S(1)} %get-tuple-element.40), channel_id=1, source_target_pairs={{0,4},{4,8},{8,12},{1,5},{5,9},{9,13},{2,6},{6,10},{10,14},{3,7},{... | collective-permute-start | bytes 12296 | tf_op jit(solution)/shard_map/ppermute | solution.py:19
  15.8 4.8 %collective-permute-start.9 = (f32[4,1,256]{2,1,0:T(1,128)S(1)}, f32[4,1,256]{2,1,0:T(1,128)S(1)}, u32[]{:S(2)}, u32[]{:S(2)}) collective-permute-start(f32[4,1,256]{2,1,0:T(1,128)S(1)} %get-tuple-element.41), channel_id=1, source_target_pairs={{4,0},{8,4},{12,8},{5,1},{9,5},{13,9},{6,2},{10,6},{14,10},{7,3},{... | collective-permute-start | bytes 12296 | tf_op jit(solution)/shard_map/ppermute | solution.py:21
  20.7 4.9 %collective-permute-start.10 = (f32[4,6,1]{2,1,0:T(8,128)S(1)}, f32[4,6,1]{2,1,0:T(8,128)S(1)}, u32[]{:S(2)}, u32[]{:S(2)}) collective-permute-start(f32[4,6,1]{2,1,0:T(8,128)S(1)} %get-tuple-element.36), channel_id=1, source_target_pairs={{0,1},{1,2},{2,3},{4,5},{5,6},{6,7},{8,9},{9,10},{10,11},{12,13},{... | collective-permute-start | bytes 296 | tf_op jit(solution)/shard_map/ppermute | solution.py:19
  24.2 5.6 %collective-permute-start.11 = (f32[4,6,1]{2,1,0:T(8,128)S(1)}, f32[4,6,1]{2,1,0:T(8,128)S(1)}, u32[]{:S(2)}, u32[]{:S(2)}) collective-permute-start(f32[4,6,1]{2,1,0:T(8,128)S(1)} %get-tuple-element.37), channel_id=1, source_target_pairs={{1,0},{2,1},{3,2},{5,4},{6,5},{7,6},{9,8},{10,9},{11,10},{13,12},{... | collective-permute-start | bytes 296 | tf_op jit(solution)/shard_map/ppermute | solution.py:21
  30.1 4.2 %collective-permute-start.2 = (bf16[16,4,1,256]{3,2,1,0:T(2,128)(2,1)S(1)}, bf16[16,4,1,256]{3,2,1,0:T(2,128)(2,1)S(1)}, u32[]{:S(2)}, u32[]{:S(2)}) collective-permute-start(bf16[16,4,1,256]{3,2,1,0:T(2,128)(2,1)S(1)} %get-tuple-element.22), channel_id=1, source_target_pairs={{0,4},{4,8},{8,12},{1,5},{5,9},{9,13},{2,6},{6,10},{10,14},{3,7},{... | collective-permute-start | bytes 98312 | tf_op jit(solution)/shard_map/ppermute | solution.py:19
  33.0 4.2 %collective-permute-start.3 = (bf16[16,4,1,256]{3,2,1,0:T(2,128)(2,1)S(1)}, bf16[16,4,1,256]{3,2,1,0:T(2,128)(2,1)S(1)}, u32[]{:S(2)}, u32[]{:S(2)}) collective-permute-start(bf16[16,4,1,256]{3,2,1,0:T(2,128)(2,1)S(1)} %get-tuple-element.23), channel_id=1, source_target_pairs={{4,0},{8,4},{12,8},{5,1},{9,5},{13,9},{6,2},{10,6},{14,10},{7,3},{... | collective-permute-start | bytes 98312 | tf_op jit(solution)/shard_map/ppermute | solution.py:21
  37.5 6.0 %collective-permute-start.4 = (bf16[16,4,6,1]{3,2,1,0:T(8,128)(2,1)S(1)}, bf16[16,4,6,1]{3,2,1,0:T(8,128)(2,1)S(1)}, u32[]{:S(2)}, u32[]{:S(2)}) collective-permute-start(bf16[16,4,6,1]{3,2,1,0:T(8,128)(2,1)S(1)} %get-tuple-element.15), channel_id=1, source_target_pairs={{0,1},{1,2},{2,3},{4,5},{5,6},{6,7},{8,9},{9,10},{10,11},{12,13},{... | collective-permute-start | bytes 2312 | tf_op jit(solution)/shard_map/ppermute | solution.py:19
  41.0 6.9 %collective-permute-start.5 = (bf16[16,4,6,1]{3,2,1,0:T(8,128)(2,1)S(1)}, bf16[16,4,6,1]{3,2,1,0:T(8,128)(2,1)S(1)}, u32[]{:S(2)}, u32[]{:S(2)}) collective-permute-start(bf16[16,4,6,1]{3,2,1,0:T(8,128)(2,1)S(1)} %get-tuple-element.14), channel_id=1, source_target_pairs={{1,0},{2,1},{3,2},{5,4},{6,5},{7,6},{9,8},{10,9},{11,10},{13,12},{... | collective-permute-start | bytes 2312 | tf_op jit(solution)/shard_map/ppermute | solution.py:21
  49.3 1.6 copy-start.1
  51.0 0.7 copy-start.2
  51.0 1.2 copy-start.3
  51.6 1.1 copy-start.4
  52.2 1.1 copy-start.5
  52.7 1.1 copy-start.6
  53.3 1.1 copy-start.7
  53.8 1.1 copy-start.8
  55.6 0.9 copy-start
  110.8 5.8 %collective-permute-start.12 = (bf16[16,1,4,256]{3,0,2,1:T(8,128)(2,1)S(1)}, bf16[16,1,4,256]{3,0,2,1:T(8,128)(2,1)S(1)}, u32[]{:S(2)}, u32[]{:S(2)}) collective-permute-start(bf16[16,1,4,256]{3,0,2,1:T(8,128)(2,1)S(1)} %get-tuple-element.24), channel_id=1, source_target_pairs={{0,16},{1,17},{2,18},{3,19},{4,20},{5,21},{6,22},{7,23},{8,24},{9,... | collective-permute-start | bytes 98312 | tf_op jit(solution)/shard_map/ppermute | solution.py:19
  115.0 5.8 %collective-permute-start.13 = (bf16[16,1,4,256]{3,0,2,1:T(8,128)(2,1)S(1)}, bf16[16,1,4,256]{3,0,2,1:T(8,128)(2,1)S(1)}, u32[]{:S(2)}, u32[]{:S(2)}) collective-permute-start(bf16[16,1,4,256]{3,0,2,1:T(8,128)(2,1)S(1)} %get-tuple-element.25), channel_id=1, source_target_pairs={{16,0},{17,1},{18,2},{19,3},{20,4},{21,5},{22,6},{23,7},{24,8},{25... | collective-permute-start | bytes 98312 | tf_op jit(solution)/shard_map/ppermute | solution.py:21
  120.8 2.6 %collective-permute-start.14 = (bf16[16,4,1,256]{3,0,2,1:T(8,128)(2,1)S(1)}, bf16[16,4,1,256]{3,0,2,1:T(8,128)(2,1)S(1)}, u32[]{:S(2)}, u32[]{:S(2)}) collective-permute-start(bf16[16,4,1,256]{3,0,2,1:T(8,128)(2,1)S(1)} %get-tuple-element.20), channel_id=1, source_target_pairs={{0,4},{4,8},{8,12},{1,5},{5,9},{9,13},{2,6},{6,10},{10,14},{3,7},{... | collective-permute-start | bytes 98312 | tf_op jit(solution)/shard_map/ppermute | solution.py:19
  122.1 3.5 %collective-permute-start.15 = (bf16[16,4,1,256]{3,0,2,1:T(8,128)(2,1)S(1)}, bf16[16,4,1,256]{3,0,2,1:T(8,128)(2,1)S(1)}, u32[]{:S(2)}, u32[]{:S(2)}) collective-permute-start(bf16[16,4,1,256]{3,0,2,1:T(8,128)(2,1)S(1)} %get-tuple-element.21), channel_id=1, source_target_pairs={{4,0},{8,4},{12,8},{5,1},{9,5},{13,9},{6,2},{10,6},{14,10},{7,3},{... | collective-permute-start | bytes 98312 | tf_op jit(solution)/shard_map/ppermute | solution.py:21
  125.7 4.5 %collective-permute-start.16 = (bf16[16,4,6,1]{3,0,2,1:T(8,128)(2,1)S(1)}, bf16[16,4,6,1]{3,0,2,1:T(8,128)(2,1)S(1)}, u32[]{:S(2)}, u32[]{:S(2)}) collective-permute-start(bf16[16,4,6,1]{3,0,2,1:T(8,128)(2,1)S(1)} %get-tuple-element.19), channel_id=1, source_target_pairs={{0,1},{1,2},{2,3},{4,5},{5,6},{6,7},{8,9},{9,10},{10,11},{12,13},{... | collective-permute-start | bytes 2312 | tf_op jit(solution)/shard_map/ppermute | solution.py:19
  128.1 6.5 %collective-permute-start.17 = (bf16[16,4,6,1]{3,0,2,1:T(8,128)(2,1)S(1)}, bf16[16,4,6,1]{3,0,2,1:T(8,128)(2,1)S(1)}, u32[]{:S(2)}, u32[]{:S(2)}) collective-permute-start(bf16[16,4,6,1]{3,0,2,1:T(8,128)(2,1)S(1)} %get-tuple-element.18), channel_id=1, source_target_pairs={{1,0},{2,1},{3,2},{5,4},{6,5},{7,6},{9,8},{10,9},{11,10},{13,12},{... | collective-permute-start | bytes 2312 | tf_op jit(solution)/shard_map/ppermute | solution.py:21
where the time goes:
time: 187 us; the launch traced here: 186 us
  blocking collectives  82.4 us (44%)
  starting transfers between devices  40 us (21%)
  waiting for transfers between devices  26.4 us (14%)
  other arithmetic  15.8 us (8%)
  matrix products  13.6 us (7%)
  local copies, waits for them, and re-layouts  6.08 us (3%)
    psum x1, blocking collectives, residual_gram(): return lax.psum(local_gram(residual, residual), ('gx', 'gy', 'gz'))  43.2 us
    psum x1, blocking collectives, on_device(): lax.psum((local_gram(direction, image), local_gram(image, residual), loca...  39.1 us
    ppermute x9, starting transfers between devices, padded_2(): lax.ppermute(tail, axis, [(i, (i + 1) % count) for i in range(ends)])  28.4 us
    ppermute x9, waiting for transfers between devices, padded_2(): lax.ppermute(head, axis, [((i + 1) % count, i) for i in range(ends)])  24.2 us
    ppermute x9, starting transfers between devices, padded_2(): lax.ppermute(head, axis, [((i + 1) % count, i) for i in range(ends)])  11.6 us
    dot_general x16, matrix products, apply_operator(): jnp.einsum('b,bcxyz->cxyz', kernel[corner], stacked, preferred_element_ty...  8.36 us
    another operation x9, other arithmetic, solve_small(): factor = jnp.linalg.cholesky(matrix)  6.4 us
    another operation x6, other arithmetic, solve_small(): return jax.scipy.linalg.cho_solve((factor, True), rhs_small)  5.63 us
  transfers between devices with their start and end apart: 18, of which 12 were waited for; matrix products, arithmetic and copies ran while one was open for 2% of the time, Pallas kernels for 0%

commit v1 on v0

--- a/solution.py
+++ b/solution.py
@@ -124,9 +124,11 @@
     current = residual_gram(residual)
     for iteration in range(ITERS):
         image = apply_operator(direction, weights, kernel)
-        curvature, cross, image_sq = lax.psum(
-            (local_gram(direction, image), local_gram(image, residual), local_gram(image, image)),
-            ("gx", "gy", "gz"),
+        carry_space = lambda t0: jax.lax.psum(
+            jax.lax.psum(t0, axis_name="gx"), axis_name=("gy", "gz")
+        )
+        curvature, cross, image_sq = carry_space(
+            (local_gram(direction, image), local_gram(image, residual), local_gram(image, image))
         )
         alpha = solve_small(curvature, current)
         solution = solution + combine(direction, alpha)

time: 187 us -> 249 us (1.33)
  blocking collectives: 82.4 us -> 143 us
  waiting for transfers between devices: 26.4 us -> 29.9 us
    psum x1 -> x4, blocking collectives: 39.1 us -> 101 us  [the longest x2 88.9 us: on_device(): jax.lax.psum(jax.lax.psum(t0, axis_name='gx'), axis_name=('gy', 'gz'))]
    ppermute x9, waiting for transfers between devices: 24.2 us -> 27.8 us  [padded_2(): lax.ppermute(head, axis, [((i + 1) % count, i) for i in range(ends)])]
  transfers between devices with their start and end apart: 18 -> 18, of which waited for: 12 -> 11; matrix products, arithmetic and copies ran while one was open for 2% -> 3% of each run, Pallas kernels for 0% -> 0%
where the time goes in v1:
time: 249 us; the launch traced here: 248 us
  blocking collectives  143 us (57%)
  starting transfers between devices  38.5 us (15%)
  waiting for transfers between devices  29.9 us (12%)
  other arithmetic  15.8 us (6%)
  matrix products  13.6 us (5%)
  local copies, waits for them, and re-layouts  6.08 us (2%)
    psum x2, blocking collectives, on_device(): jax.lax.psum(jax.lax.psum(t0, axis_name='gx'), axis_name=('gy', 'gz'))  88.9 us
    psum x1, blocking collectives, residual_gram(): return lax.psum(local_gram(residual, residual), ('gx', 'gy', 'gz'))  41.7 us
    ppermute x9, waiting for transfers between devices, padded_2(): lax.ppermute(head, axis, [((i + 1) % count, i) for i in range(ends)])  27.8 us
    ppermute x9, starting transfers between devices, padded_2(): lax.ppermute(tail, axis, [(i, (i + 1) % count) for i in range(ends)])  26.9 us
    psum x2, blocking collectives, on_device(): jax.lax.psum(t0, axis_name='gx')  12.4 us
    ppermute x9, starting transfers between devices, padded_2(): lax.ppermute(head, axis, [((i + 1) % count, i) for i in range(ends)])  11.6 us
    dot_general x16, matrix products, apply_operator(): jnp.einsum('b,bcxyz->cxyz', kernel[corner], stacked, preferred_element_ty...  8.39 us
    another operation x9, other arithmetic, solve_small(): factor = jnp.linalg.cholesky(matrix)  6.39 us
  transfers between devices with their start and end apart: 18, of which 11 were waited for; matrix products, arithmetic and copies ran while one was open for 3% of the time, Pallas kernels for 0%

profile of v1, /device:TPU:0, one launch (start us, length us, event | category | flops | bytes accessed | tf_op | source)
XLA Modules:
  0.0 248.3 jit_solution(6272701478678985922)
XLA Ops:
  0.6 0.9 convert_element_type.9
  1.6 4.9 %collective-permute-start = (bf16[16,1,4,256]{3,2,1,0:T(4,128)(2,1)S(1)}, bf16[16,1,4,256]{3,2,1,0:T(4,128)(2,1)S(1)}, u32[]{:S(2)}, u32[]{:S(2)}) collective-permute-start(bf16[16,1,4,256]{3,2,1,0:T(4,128)(2,1)S(1)} %get-tuple-element.28), channel_id=1, source_target_pairs={{0,16},{1,17},{2,18},{3,19},{4,20},{5,21},{6,22},{7,23},{8,24},{9,... | collective-permute-start | bytes 98312 | tf_op jit(solution)/shard_map/ppermute | solution.py:19
  6.5 1.3 collective-permute-start.1
  7.8 0.8 select_reduce_fusion
  8.6 4.5 %collective-permute-start.6 = (f32[1,4,256]{2,1,0:T(4,128)S(1)}, f32[1,4,256]{2,1,0:T(4,128)S(1)}, u32[]{:S(2)}, u32[]{:S(2)}) collective-permute-start(f32[1,4,256]{2,1,0:T(4,128)S(1)} %get-tuple-element.44), channel_id=1, source_target_pairs={{0,16},{1,17},{2,18},{3,19},{4,20},{5,21},{6,22},{7,23},{8,24},{9,... | collective-permute-start | bytes 12296 | tf_op jit(solution)/shard_map/ppermute | solution.py:19
  13.2 1.3 collective-permute-start.7
  14.5 1.3 convolution_bitcast_fusion.4
  15.7 41.7 %psum.65 = f32[16,16]{0,1:T(8,128)S(1)} all-reduce(f32[16,16]{0,1:T(8,128)S(1)} %convolution_bitcast_fusion.4), channel_id=1, replica_groups=mesh['gx'=2,'gy'=4,'gz'=4] {'gx','gy','gz'}, use_global_device_ids=true, to_apply=%region_5.0 | all-reduce | flops 256 | bytes 2048 | tf_op jit(solution)/shard_map/psum | solution.py:102
  57.5 1.5 cholesky.70
  59.0 0.6 compare_reduce_fusion.1
  59.7 1.3 collective-permute-start.8
  60.9 1.3 collective-permute-start.9
  62.2 0.7 fusion.56
  62.9 1.2 custom-call.10
  64.1 2.4 collective-permute-done.9
  66.6 3.4 %collective-permute-start.10 = (f32[4,6,1]{2,1,0:T(8,128)S(1)}, f32[4,6,1]{2,1,0:T(8,128)S(1)}, u32[]{:S(2)}, u32[]{:S(2)}) collective-permute-start(f32[4,6,1]{2,1,0:T(8,128)S(1)} %get-tuple-element.38), channel_id=1, source_target_pairs={{0,1},{1,2},{2,3},{4,5},{5,6},{6,7},{8,9},{9,10},{10,11},{12,13},{... | collective-permute-start | bytes 296 | tf_op jit(solution)/shard_map/ppermute | solution.py:19
  70.0 1.3 collective-permute-start.11
  71.4 4.2 %collective-permute-done.11 = f32[4,6,1]{2,1,0:T(8,128)S(1)} collective-permute-done((f32[4,6,1]{2,1,0:T(8,128)S(1)}, f32[4,6,1]{2,1,0:T(8,128)S(1)}, u32[]{:S(2)}, u32[]{:S(2)}) %collective-permute-start.11) | collective-permute-done | bytes 128 | tf_op jit(solution)/shard_map/ppermute | solution.py:21
  76.0 2.8 %collective-permute-start.2 = (bf16[16,4,1,256]{3,2,1,0:T(2,128)(2,1)S(1)}, bf16[16,4,1,256]{3,2,1,0:T(2,128)(2,1)S(1)}, u32[]{:S(2)}, u32[]{:S(2)}) collective-permute-start(bf16[16,4,1,256]{3,2,1,0:T(2,128)(2,1)S(1)} %get-tuple-element.24), channel_id=1, source_target_pairs={{0,4},{4,8},{8,12},{1,5},{5,9},{9,13},{2,6},{6,10},{10,14},{3,7},{... | collective-permute-start | bytes 98312 | tf_op jit(solution)/shard_map/ppermute | solution.py:19
  78.8 1.3 collective-permute-start.3
  80.2 3.4 %collective-permute-done.3 = bf16[16,4,1,256]{3,2,1,0:T(2,128)(2,1)S(1)} collective-permute-done((bf16[16,4,1,256]{3,2,1,0:T(2,128)(2,1)S(1)}, bf16[16,4,1,256]{3,2,1,0:T(2,128)(2,1)S(1)}, u32[]{:S(2)}, u32[]{:S(2)}) %collective-permute-start.3) | collective-permute-done | bytes 32800 | tf_op jit(solution)/shard_map/ppermute | solution.py:21
  83.9 3.3 %collective-permute-start.4 = (bf16[16,4,6,1]{3,2,1,0:T(8,128)(2,1)S(1)}, bf16[16,4,6,1]{3,2,1,0:T(8,128)(2,1)S(1)}, u32[]{:S(2)}, u32[]{:S(2)}) collective-permute-start(bf16[16,4,6,1]{3,2,1,0:T(8,128)(2,1)S(1)} %get-tuple-element.17), channel_id=1, source_target_pairs={{0,1},{1,2},{2,3},{4,5},{5,6},{6,7},{8,9},{9,10},{10,11},{12,13},{... | collective-permute-start | bytes 2312 | tf_op jit(solution)/shard_map/ppermute | solution.py:19
  87.2 1.3 collective-permute-start.5
  88.6 1.1 collective-permute-done.4
  89.7 4.4 %collective-permute-done.5 = bf16[16,4,6,1]{3,2,1,0:T(8,128)(2,1)S(1)} collective-permute-done((bf16[16,4,6,1]{3,2,1,0:T(8,128)(2,1)S(1)}, bf16[16,4,6,1]{3,2,1,0:T(8,128)(2,1)S(1)}, u32[]{:S(2)}, u32[]{:S(2)}) %collective-permute-start.5) | collective-permute-done | bytes 800 | tf_op jit(solution)/shard_map/ppermute | solution.py:21
  94.1 0.9 pad_maximum_fusion
  95.5 1.6 copy.46
  97.2 0.5 fusion.82
  97.8 0.5 fusion.83
  98.4 0.5 fusion.84
  99.0 0.5 fusion.85
  99.5 0.5 fusion.86
  100.1 0.5 fusion.87
  100.6 0.5 fusion.88
  101.1 0.5 fusion.89
  102.0 0.8 copy-done
  103.5 7.4 %all-reduce.1 = (f32[16,16]{0,1:T(8,128)S(1)}, f32[16,16]{1,0:T(8,128)S(1)}, f32[16,16]{1,0:T(8,128)S(1)}) all-reduce(f32[16,16]{0,1:T(8,128)S(1)} %bitcast.265, f32[16,16]{1,0:T(8,128)S(1)} %convolution_bitcast_fusion.3, f32[16,16]{1,0:T(8,128)S(1)} %bitcast.266), channel_id=1, replica_groups=mesh['gx'=2,'gy'=4,'gz'=4] {'gx'}, use_global_device_ids=true, to_apply=%region_1.2 | all-reduce | flops 768 | bytes 6144 | tf_op jit(solution)/shard_map/psum | solution.py:128
  110.9 58.2 %all-reduce = (f32[16,16]{0,1:T(8,128)S(1)}, f32[16,16]{1,0:T(8,128)S(1)}, f32[16,16]{1,0:T(8,128)S(1)}) all-reduce(f32[16,16]{0,1:T(8,128)S(1)} %get-tuple-element.11, f32[16,16]{1,0:T(8,128)S(1)} %get-tuple-element.12, f32[16,16]{1,0:T(8,128)S(1)} %get-tuple-element.13), channel_id=1, replica_groups=mesh['gx'=2,'gy'=4,'gz'=4] {'gy','gz'}, use_global_device_ids=true, to_apply=%region_2.3 | all-reduce | flops 768 | bytes 6144 | tf_op jit(solution)/shard_map/psum | solution.py:127
  169.2 1.5 cholesky.59
  170.7 0.6 compare_reduce_fusion.2
  171.4 0.6 fusion.55
  172.0 1.2 custom-call.9
  175.3 3.4 %collective-permute-start.12 = (bf16[16,1,4,256]{3,0,2,1:T(8,128)(2,1)S(1)}, bf16[16,1,4,256]{3,0,2,1:T(8,128)(2,1)S(1)}, u32[]{:S(2)}, u32[]{:S(2)}) collective-permute-start(bf16[16,1,4,256]{3,0,2,1:T(8,128)(2,1)S(1)} %get-tuple-element.26), channel_id=1, source_target_pairs={{0,16},{1,17},{2,18},{3,19},{4,20},{5,21},{6,22},{7,23},{8,24},{9,... | collective-permute-start | bytes 98312 | tf_op jit(solution)/shard_map/ppermute | solution.py:19
  178.7 1.3 collective-permute-start.13
  180.3 4.2 %collective-permute-done.13 = bf16[16,1,4,256]{3,0,2,1:T(8,128)(2,1)S(1)} collective-permute-done((bf16[16,1,4,256]{3,0,2,1:T(8,128)(2,1)S(1)}, bf16[16,1,4,256]{3,0,2,1:T(8,128)(2,1)S(1)}, u32[]{:S(2)}, u32[]{:S(2)}) %collective-permute-start.13) | collective-permute-done | bytes 32800 | tf_op jit(solution)/shard_map/ppermute | solution.py:21
  184.5 1.3 collective-permute-start.14
  185.8 1.3 collective-permute-start.15
  187.2 4.9 %collective-permute-done.15 = bf16[16,4,1,256]{3,0,2,1:T(8,128)(2,1)S(1)} collective-permute-done((bf16[16,4,1,256]{3,0,2,1:T(8,128)(2,1)S(1)}, bf16[16,4,1,256]{3,0,2,1:T(8,128)(2,1)S(1)}, u32[]{:S(2)}, u32[]{:S(2)}) %collective-permute-start.15) | collective-permute-done | bytes 32800 | tf_op jit(solution)/shard_map/ppermute | solution.py:21
  192.2 1.9 collective-permute-start.16
  194.1 1.3 collective-permute-start.17
  195.7 0.6 collective-permute-done.16
  196.3 4.3 %collective-permute-done.17 = bf16[16,4,6,1]{3,0,2,1:T(8,128)(2,1)S(1)} collective-permute-done((bf16[16,4,6,1]{3,0,2,1:T(8,128)(2,1)S(1)}, bf16[16,4,6,1]{3,0,2,1:T(8,128)(2,1)S(1)}, u32[]{:S(2)}, u32[]{:S(2)}) %collective-permute-start.17) | collective-permute-done | bytes 800 | tf_op jit(solution)/shard_map/ppermute | solution.py:21
  201.6 0.5 fusion.10
  202.1 0.5 fusion.12
  203.7 0.5 fusion.18
  204.3 0.5 fusion.20
  206.1 5.0 %psum.70 = f32[16,16]{0,1:T(8,128)S(1)} all-reduce(f32[16,16]{0,1:T(8,128)S(1)} %convolution_bitcast_fusion.1), channel_id=1, replica_groups=mesh['gx'=2,'gy'=4,'gz'=4] {'gx'}, use_global_device_ids=true, to_apply=%region_10.13 | all-reduce | flops 256 | bytes 2048 | tf_op jit(solution)/shard_map/psum | solution.py:128
  211.1 30.6 %psum.71 = f32[16,16]{0,1:T(8,128)S(1)} all-reduce(f32[16,16]{0,1:T(8,128)S(1)} %psum.70), channel_id=1, replica_groups=mesh['gx'=2,'gy'=4,'gz'=4] {'gy','gz'}, use_global_device_ids=true, to_apply=%region_11.14 | all-reduce | flops 256 | bytes 2048 | tf_op jit(solution)/shard_map/psum | solution.py:127
  241.8 1.5 cholesky.81
  243.3 0.6 compare_reduce_fusion
  244.0 0.6 fusion.57
  244.6 1.2 custom-call.11
  246.5 0.7 copy.45
  247.5 0.7 copy.44
  (104 shorter events, 10.0 us)
Async XLA Ops:
  1.6 74.2 %collective-permute-start = (bf16[16,1,4,256]{3,2,1,0:T(4,128)(2,1)S(1)}, bf16[16,1,4,256]{3,2,1,0:T(4,128)(2,1)S(1)}, u32[]{:S(2)}, u32[]{:S(2)}) collective-permute-start(bf16[16,1,4,256]{3,2,1,0:T(4,128)(2,1)S(1)} %get-tuple-element.28), channel_id=1, source_target_pairs={{0,16},{1,17},{2,18},{3,19},{4,20},{5,21},{6,22},{7,23},{8,24},{9,... | collective-permute-start | bytes 98312 | tf_op jit(solution)/shard_map/ppermute | solution.py:19
  6.5 69.3 %collective-permute-start.1 = (bf16[16,1,4,256]{3,2,1,0:T(4,128)(2,1)S(1)}, bf16[16,1,4,256]{3,2,1,0:T(4,128)(2,1)S(1)}, u32[]{:S(2)}, u32[]{:S(2)}) collective-permute-start(bf16[16,1,4,256]{3,2,1,0:T(4,128)(2,1)S(1)} %get-tuple-element.29), channel_id=1, source_target_pairs={{16,0},{17,1},{18,2},{19,3},{20,4},{21,5},{22,6},{23,7},{24,8},{25... | collective-permute-start | bytes 98312 | tf_op jit(solution)/shard_map/ppermute | solution.py:21
  8.6 51.0 %collective-permute-start.6 = (f32[1,4,256]{2,1,0:T(4,128)S(1)}, f32[1,4,256]{2,1,0:T(4,128)S(1)}, u32[]{:S(2)}, u32[]{:S(2)}) collective-permute-start(f32[1,4,256]{2,1,0:T(4,128)S(1)} %get-tuple-element.44), channel_id=1, source_target_pairs={{0,16},{1,17},{2,18},{3,19},{4,20},{5,21},{6,22},{7,23},{8,24},{9,... | collective-permute-start | bytes 12296 | tf_op jit(solution)/shard_map/ppermute | solution.py:19
  13.2 46.5 %collective-permute-start.7 = (f32[1,4,256]{2,1,0:T(4,128)S(1)}, f32[1,4,256]{2,1,0:T(4,128)S(1)}, u32[]{:S(2)}, u32[]{:S(2)}) collective-permute-start(f32[1,4,256]{2,1,0:T(4,128)S(1)} %get-tuple-element.45), channel_id=1, source_target_pairs={{16,0},{17,1},{18,2},{19,3},{20,4},{21,5},{22,6},{23,7},{24,8},{25... | collective-permute-start | bytes 12296 | tf_op jit(solution)/shard_map/ppermute | solution.py:21
  59.7 4.5 %collective-permute-start.8 = (f32[4,1,256]{2,1,0:T(1,128)S(1)}, f32[4,1,256]{2,1,0:T(1,128)S(1)}, u32[]{:S(2)}, u32[]{:S(2)}) collective-permute-start(f32[4,1,256]{2,1,0:T(1,128)S(1)} %get-tuple-element.42), channel_id=1, source_target_pairs={{0,4},{4,8},{8,12},{1,5},{5,9},{9,13},{2,6},{6,10},{10,14},{3,7},{... | collective-permute-start | bytes 12296 | tf_op jit(solution)/shard_map/ppermute | solution.py:19
  60.9 5.6 %collective-permute-start.9 = (f32[4,1,256]{2,1,0:T(1,128)S(1)}, f32[4,1,256]{2,1,0:T(1,128)S(1)}, u32[]{:S(2)}, u32[]{:S(2)}) collective-permute-start(f32[4,1,256]{2,1,0:T(1,128)S(1)} %get-tuple-element.43), channel_id=1, source_target_pairs={{4,0},{8,4},{12,8},{5,1},{9,5},{13,9},{6,2},{10,6},{14,10},{7,3},{... | collective-permute-start | bytes 12296 | tf_op jit(solution)/shard_map/ppermute | solution.py:21
  66.6 4.8 %collective-permute-start.10 = (f32[4,6,1]{2,1,0:T(8,128)S(1)}, f32[4,6,1]{2,1,0:T(8,128)S(1)}, u32[]{:S(2)}, u32[]{:S(2)}) collective-permute-start(f32[4,6,1]{2,1,0:T(8,128)S(1)} %get-tuple-element.38), channel_id=1, source_target_pairs={{0,1},{1,2},{2,3},{4,5},{5,6},{6,7},{8,9},{9,10},{10,11},{12,13},{... | collective-permute-start | bytes 296 | tf_op jit(solution)/shard_map/ppermute | solution.py:19
  70.0 5.6 %collective-permute-start.11 = (f32[4,6,1]{2,1,0:T(8,128)S(1)}, f32[4,6,1]{2,1,0:T(8,128)S(1)}, u32[]{:S(2)}, u32[]{:S(2)}) collective-permute-start(f32[4,6,1]{2,1,0:T(8,128)S(1)} %get-tuple-element.39), channel_id=1, source_target_pairs={{1,0},{2,1},{3,2},{5,4},{6,5},{7,6},{9,8},{10,9},{11,10},{13,12},{... | collective-permute-start | bytes 296 | tf_op jit(solution)/shard_map/ppermute | solution.py:21
  76.0 4.2 %collective-permute-start.2 = (bf16[16,4,1,256]{3,2,1,0:T(2,128)(2,1)S(1)}, bf16[16,4,1,256]{3,2,1,0:T(2,128)(2,1)S(1)}, u32[]{:S(2)}, u32[]{:S(2)}) collective-permute-start(bf16[16,4,1,256]{3,2,1,0:T(2,128)(2,1)S(1)} %get-tuple-element.24), channel_id=1, source_target_pairs={{0,4},{4,8},{8,12},{1,5},{5,9},{9,13},{2,6},{6,10},{10,14},{3,7},{... | collective-permute-start | bytes 98312 | tf_op jit(solution)/shard_map/ppermute | solution.py:19
  78.8 4.7 %collective-permute-start.3 = (bf16[16,4,1,256]{3,2,1,0:T(2,128)(2,1)S(1)}, bf16[16,4,1,256]{3,2,1,0:T(2,128)(2,1)S(1)}, u32[]{:S(2)}, u32[]{:S(2)}) collective-permute-start(bf16[16,4,1,256]{3,2,1,0:T(2,128)(2,1)S(1)} %get-tuple-element.25), channel_id=1, source_target_pairs={{4,0},{8,4},{12,8},{5,1},{9,5},{13,9},{6,2},{10,6},{14,10},{7,3},{... | collective-permute-start | bytes 98312 | tf_op jit(solution)/shard_map/ppermute | solution.py:21
  83.9 5.8 %collective-permute-start.4 = (bf16[16,4,6,1]{3,2,1,0:T(8,128)(2,1)S(1)}, bf16[16,4,6,1]{3,2,1,0:T(8,128)(2,1)S(1)}, u32[]{:S(2)}, u32[]{:S(2)}) collective-permute-start(bf16[16,4,6,1]{3,2,1,0:T(8,128)(2,1)S(1)} %get-tuple-element.17), channel_id=1, source_target_pairs={{0,1},{1,2},{2,3},{4,5},{5,6},{6,7},{8,9},{9,10},{10,11},{12,13},{... | collective-permute-start | bytes 2312 | tf_op jit(solution)/shard_map/ppermute | solution.py:19
  87.2 6.9 %collective-permute-start.5 = (bf16[16,4,6,1]{3,2,1,0:T(8,128)(2,1)S(1)}, bf16[16,4,6,1]{3,2,1,0:T(8,128)(2,1)S(1)}, u32[]{:S(2)}, u32[]{:S(2)}) collective-permute-start(bf16[16,4,6,1]{3,2,1,0:T(8,128)(2,1)S(1)} %get-tuple-element.16), channel_id=1, source_target_pairs={{1,0},{2,1},{3,2},{5,4},{6,5},{7,6},{9,8},{10,9},{11,10},{13,12},{... | collective-permute-start | bytes 2312 | tf_op jit(solution)/shard_map/ppermute | solution.py:21
  95.5 1.6 copy-start.1
  97.2 0.7 copy-start.2
  97.2 1.2 copy-start.3
  97.8 1.1 copy-start.4
  98.4 1.1 copy-start.5
  98.9 1.1 copy-start.6
  99.5 1.1 copy-start.7
  100.1 1.1 copy-start.8
  101.8 0.9 copy-start
  175.3 5.0 %collective-permute-start.12 = (bf16[16,1,4,256]{3,0,2,1:T(8,128)(2,1)S(1)}, bf16[16,1,4,256]{3,0,2,1:T(8,128)(2,1)S(1)}, u32[]{:S(2)}, u32[]{:S(2)}) collective-permute-start(bf16[16,1,4,256]{3,0,2,1:T(8,128)(2,1)S(1)} %get-tuple-element.26), channel_id=1, source_target_pairs={{0,16},{1,17},{2,18},{3,19},{4,20},{5,21},{6,22},{7,23},{8,24},{9,... | collective-permute-start | bytes 98312 | tf_op jit(solution)/shard_map/ppermute | solution.py:19
  178.7 5.8 %collective-permute-start.13 = (bf16[16,1,4,256]{3,0,2,1:T(8,128)(2,1)S(1)}, bf16[16,1,4,256]{3,0,2,1:T(8,128)(2,1)S(1)}, u32[]{:S(2)}, u32[]{:S(2)}) collective-permute-start(bf16[16,1,4,256]{3,0,2,1:T(8,128)(2,1)S(1)} %get-tuple-element.27), channel_id=1, source_target_pairs={{16,0},{17,1},{18,2},{19,3},{20,4},{21,5},{22,6},{23,7},{24,8},{25... | collective-permute-start | bytes 98312 | tf_op jit(solution)/shard_map/ppermute | solution.py:21
  184.5 2.6 %collective-permute-start.14 = (bf16[16,4,1,256]{3,0,2,1:T(8,128)(2,1)S(1)}, bf16[16,4,1,256]{3,0,2,1:T(8,128)(2,1)S(1)}, u32[]{:S(2)}, u32[]{:S(2)}) collective-permute-start(bf16[16,4,1,256]{3,0,2,1:T(8,128)(2,1)S(1)} %get-tuple-element.22), channel_id=1, source_target_pairs={{0,4},{4,8},{8,12},{1,5},{5,9},{9,13},{2,6},{6,10},{10,14},{3,7},{... | collective-permute-start | bytes 98312 | tf_op jit(solution)/shard_map/ppermute | solution.py:19
  185.8 6.2 %collective-permute-start.15 = (bf16[16,4,1,256]{3,0,2,1:T(8,128)(2,1)S(1)}, bf16[16,4,1,256]{3,0,2,1:T(8,128)(2,1)S(1)}, u32[]{:S(2)}, u32[]{:S(2)}) collective-permute-start(bf16[16,4,1,256]{3,0,2,1:T(8,128)(2,1)S(1)} %get-tuple-element.23), channel_id=1, source_target_pairs={{4,0},{8,4},{12,8},{5,1},{9,5},{13,9},{6,2},{10,6},{14,10},{7,3},{... | collective-permute-start | bytes 98312 | tf_op jit(solution)/shard_map/ppermute | solution.py:21
  192.2 4.1 %collective-permute-start.16 = (bf16[16,4,6,1]{3,0,2,1:T(8,128)(2,1)S(1)}, bf16[16,4,6,1]{3,0,2,1:T(8,128)(2,1)S(1)}, u32[]{:S(2)}, u32[]{:S(2)}) collective-permute-start(bf16[16,4,6,1]{3,0,2,1:T(8,128)(2,1)S(1)} %get-tuple-element.21), channel_id=1, source_target_pairs={{0,1},{1,2},{2,3},{4,5},{5,6},{6,7},{8,9},{9,10},{10,11},{12,13},{... | collective-permute-start | bytes 2312 | tf_op jit(solution)/shard_map/ppermute | solution.py:19
  194.1 6.5 %collective-permute-start.17 = (bf16[16,4,6,1]{3,0,2,1:T(8,128)(2,1)S(1)}, bf16[16,4,6,1]{3,0,2,1:T(8,128)(2,1)S(1)}, u32[]{:S(2)}, u32[]{:S(2)}) collective-permute-start(bf16[16,4,6,1]{3,0,2,1:T(8,128)(2,1)S(1)} %get-tuple-element.20), channel_id=1, source_target_pairs={{1,0},{2,1},{3,2},{5,4},{6,5},{7,6},{9,8},{10,9},{11,10},{13,12},{... | collective-permute-start | bytes 2312 | tf_op jit(solution)/shard_map/ppermute | solution.py:21
